TPU v7x, 32 devices: a whole 2x2x4 slice. The times are simulated.
32 devices in a mesh: layer: 2 (over core), row: 16 (over z, y, x).
Axes of the slice: x: 2, y: 2, z: 4, core: 2. Of those that a mesh axis runs over, the one named last changes fastest.
Arguments:
- sources: bfloat16 [2, 4608, 512], P('layer', 'row'), may hold values from -2 to 2
- green_down: bfloat16 [2, 4608, 4608], P('layer', 'row')
- green_up: bfloat16 [2, 4608, 4608], P('layer', 'row')
- material: int32 [8, 4608], P('layer', 'row'), may hold values 0 or 1
- pml_cells: int32 [1], replicated, may hold values from 4 to 39
Outputs:
- residual: bfloat16 [8, 4608, 512], P('layer', 'row')
All inputs are finite; a program needn't handle non-finite values. No bound on the sum of `material` on one device may be relied on, other than what follows from the above.
Results may differ from a plain program's by a relative error of at most 0.005.
Values may be sent and summed in bfloat16 or wider, within the bound.
No kernel may reach another device: no remote copies, remote signals or barrier semaphores. Data moves between devices by JAX's collectives and lax.ppermute only.
A program may use at most 64 MiB of HBM per device.

v0:
```python
import jax
import jax.numpy as jnp
from jax import lax
from jax.sharding import PartitionSpec as P

BS = 256


def shifted(value, axis, steps):
    count = lax.axis_size(axis)
    leading, last = (max(0, -steps), min(count, count - steps))
    return lax.ppermute(value, axis, [(source, source + steps) for source in range(leading, last)])


def with_halo(cells, sides, width):
    for axis, dim in sides:
        count = lax.axis_size(axis)
        ends = count - 1
        head = lax.slice_in_dim(cells, 0, width, axis=dim)
        tail = lax.slice_in_dim(cells, cells.shape[dim] - width, cells.shape[dim], axis=dim)
        cells = jnp.concatenate(
            [
                lax.ppermute(tail, axis, [(i, (i + 1) % count) for i in range(ends)]),
                cells,
                lax.ppermute(head, axis, [((i + 1) % count, i) for i in range(ends)]),
            ],
            axis=dim,
        )
    return cells


def take_down(last):
    return shifted(last, "layer", 1)


def take_up(last):
    return shifted(last, "layer", -1)


def folder(matrix, active, total, piece):
    return lax.cond(
        active, lambda: jnp.dot(matrix, piece, preferred_element_type=jnp.float32), lambda: total
    )


def ramp(index, count, thick):
    dist = jnp.minimum(index, count - 1 - index).astype(jnp.float32)
    return jnp.maximum(thick - dist, 0.0) / thick


def local(sources, green_down, green_up, material, pml_cells):
    source = sources[0]
    down_matrix = green_down[0]
    up_matrix = green_up[0]
    rows, total = source.shape
    layers = lax.axis_size("layer")
    here = lax.axis_index("layer")
    batches = total // BS
    width = total // batches
    ticks = layers + batches - 1

    def store(buffer, result, active, start, size):
        old = lax.dynamic_slice_in_dim(buffer, start, size, 1)
        return lax.dynamic_update_slice_in_dim(buffer, jnp.where(active, result, old), start, 1)

    up_rank = layers - 1 - here
    empty = jnp.zeros((rows, width), jnp.float32)
    blank = jnp.zeros((rows, width), jnp.bfloat16)
    store_init = jnp.zeros((rows, total), jnp.bfloat16)

    def inputs(incoming, tick, rank):
        batch = tick - rank
        active = jnp.logical_and(batch >= 0, batch < batches)
        start = jnp.clip(batch, 0, batches - 1) * width
        piece = lax.dynamic_slice_in_dim(source, start, width, 1)
        entry = (piece.astype(jnp.float32) + incoming.astype(jnp.float32)).astype(jnp.bfloat16)
        return (entry, active, start)

    def both_step(tick, state):
        last_down, last_up, buffer_down, buffer_up = state
        entry_down, active_down, start_down = inputs(take_down(last_down), tick, here)
        entry_up, active_up, start_up = inputs(take_up(last_up), tick, up_rank)
        sum_down = folder(
            down_matrix, active_down, empty, lax.all_gather(entry_down, "row", axis=0, tiled=True)
        )
        sum_up = folder(
            up_matrix, active_up, empty, lax.all_gather(entry_up, "row", axis=0, tiled=True)
        )
        result_down = sum_down.astype(jnp.bfloat16)
        result_up = sum_up.astype(jnp.bfloat16)
        return (
            result_down,
            result_up,
            store(buffer_down, result_down, active_down, start_down, width),
            store(buffer_up, result_up, active_up, start_up, width),
        )

    final = lax.fori_loop(0, ticks, both_step, (blank, blank, store_init, store_init))
    down = final[2]
    up = final[3]
    wave = source.astype(jnp.float32) + down.astype(jnp.float32) + up.astype(jnp.float32)
    planes = material.shape[0]
    factor = (planes - jnp.arange(planes, dtype=jnp.float32)) / planes
    slab = wave[None, :, :] * factor[:, None, None]
    thick = pml_cells[0].astype(jnp.float32)
    plane_index = here * planes + jnp.arange(planes, dtype=jnp.int32)
    point_index = lax.axis_index("row") * rows + jnp.arange(rows, dtype=jnp.int32)
    ramp_z = ramp(plane_index, layers * planes, thick)
    ramp_m = ramp(point_index, rows * lax.axis_size("row"), thick)
    sigma = 3.0 * (ramp_z[:, None] * ramp_z[:, None] + ramp_m[None, :] * ramp_m[None, :])
    kappa = 1.0 + 1.5 * material.astype(jnp.float32)
    padded = with_halo(slab.astype(jnp.bfloat16), (("layer", 0), ("row", 1)), 1).astype(slab.dtype)
    beside = padded[2:, 1:-1] + padded[:-2, 1:-1] + padded[1:-1, 2:] + padded[1:-1, :-2]
    result = kappa[:, :, None] * ((4.0 + sigma)[:, :, None] * slab - beside)
    return result.astype(jnp.bfloat16)


def solution(mesh):
    return jax.shard_map(
        local,
        mesh=mesh,
        in_specs=(
            P("layer", "row", None),
            P("layer", "row", None),
            P("layer", "row", None),
            P("layer", "row"),
            P(),
        ),
        out_specs=P("layer", "row", None),
        check_vma=False,
    )
```

profile of v0, /device:TPU:6, one launch (start us, length us, event | category | flops | bytes accessed | tf_op | source)
XLA Modules:
  0.0 442.8 jit_solution(9857693891197550691)
XLA Ops:
  6.6 0.7 broadcast_in_dim.10
  7.3 405.5 %while.19 = (s32[]{:T(128)}, bf16[288,256]{1,0:T(8,128)(2,1)}, bf16[288,256]{1,0:T(8,128)(2,1)S(1)}, bf16[288,512]{1,0:T(8,128)(2,1)S(1)}, bf16[288,512]{1,0:T(8...) while((s32[]{:T(128)}, bf16[288,256]{1,0:T(8,128)(2,1)}, ...), condition=%wide.region_5.6_spmd, body=%wide.region_0.5_spmd.sunk | while | flops 1359839232 | bytes 40108696 | solution.py:98
  7.3 0.0 all-gather.5.cloned.1.call-start
  7.3 1.3 collective-permute-start
  8.7 3.0 collective-permute-start.1
  11.7 0.0 collective-permute-done
  11.7 1.2 collective-permute-done.1
  12.9 1.8 add_convert_fusion.3
  14.7 0.0 all-gather.5.cloned.1.call-update
  14.7 0.0 all-gather.3.cloned.1.call-start
  14.7 0.7 all-gather.3.cloned.1.call-update
  15.4 61.9 %all-gather.5.cloned.1.call-done = bf16[4608,256]{1,0:T(8,128)(2,1)} async-done(((bf16[288,256]{1,0:T(8,128)(2,1)}), bf16[4608,256]{1,0:T(8,128)(2,1)}) %all-gather.5.cloned.1.call-update) | async-done | bytes 2359312 | tf_op jit(solution)/shard_map/while/body/eval_jaxpr/all_gather | solution.py:87
  77.3 0.7 copy-done
  78.1 62.7 %all-gather.3.cloned.1.call-done = bf16[4608,256]{1,0:T(8,128)(2,1)} async-done(((bf16[288,256]{1,0:T(8,128)(2,1)}), bf16[4608,256]{1,0:T(8,128)(2,1)}) %all-gather.3.cloned.1.call-update) | async-done | bytes 2359312 | tf_op jit(solution)/shard_map/while/body/eval_jaxpr/all_gather | solution.py:84
  140.7 3.2 conditional.4
  140.7 3.2 convolution_convert_fusion
  143.9 1.0 select_dynamic-update-slice_fusion.4
  144.9 0.0 all-gather.5.cloned.1.call-start
  145.0 1.3 collective-permute-start
  146.3 3.0 collective-permute-start.1
  149.3 0.0 collective-permute-done
  149.3 1.2 collective-permute-done.1
  150.5 1.8 add_convert_fusion.3
  152.2 0.0 all-gather.5.cloned.1.call-update
  152.3 0.0 all-gather.3.cloned.1.call-start
  152.3 0.5 all-gather.3.cloned.1.call-update
  152.9 60.1 %all-gather.5.cloned.1.call-done = bf16[4608,256]{1,0:T(8,128)(2,1)} async-done(((bf16[288,256]{1,0:T(8,128)(2,1)}), bf16[4608,256]{1,0:T(8,128)(2,1)}) %all-gather.5.cloned.1.call-update) | async-done | bytes 2359312 | tf_op jit(solution)/shard_map/while/body/eval_jaxpr/all_gather | solution.py:87
  213.0 3.5 conditional.5
  213.0 3.5 convolution_convert_fusion.1
  216.5 0.7 copy-done
  217.1 1.0 select_dynamic-update-slice_fusion.5
  218.1 58.2 %all-gather.3.cloned.1.call-done = bf16[4608,256]{1,0:T(8,128)(2,1)} async-done(((bf16[288,256]{1,0:T(8,128)(2,1)}), bf16[4608,256]{1,0:T(8,128)(2,1)}) %all-gather.3.cloned.1.call-update) | async-done | bytes 2359312 | tf_op jit(solution)/shard_map/while/body/eval_jaxpr/all_gather | solution.py:84
  276.3 3.2 conditional.4
  276.3 3.2 convolution_convert_fusion
  279.5 1.0 select_dynamic-update-slice_fusion.4
  280.5 0.0 all-gather.5.cloned.1.call-start
  280.5 1.3 collective-permute-start
  281.8 3.0 collective-permute-start.1
  284.9 1.2 collective-permute-done.1
  286.0 1.8 add_convert_fusion.3
  287.8 0.0 all-gather.5.cloned.1.call-update
  287.8 0.0 all-gather.3.cloned.1.call-start
  287.9 0.5 all-gather.3.cloned.1.call-update
  288.4 60.1 %all-gather.5.cloned.1.call-done = bf16[4608,256]{1,0:T(8,128)(2,1)} async-done(((bf16[288,256]{1,0:T(8,128)(2,1)}), bf16[4608,256]{1,0:T(8,128)(2,1)}) %all-gather.5.cloned.1.call-update) | async-done | bytes 2359312 | tf_op jit(solution)/shard_map/while/body/eval_jaxpr/all_gather | solution.py:87
  348.6 3.5 conditional.5
  348.6 3.5 convolution_convert_fusion.1
  352.0 0.7 copy-done
  352.7 1.0 select_dynamic-update-slice_fusion.5
  353.7 58.2 %all-gather.3.cloned.1.call-done = bf16[4608,256]{1,0:T(8,128)(2,1)} async-done(((bf16[288,256]{1,0:T(8,128)(2,1)}), bf16[4608,256]{1,0:T(8,128)(2,1)}) %all-gather.3.cloned.1.call-update) | async-done | bytes 2359312 | tf_op jit(solution)/shard_map/while/body/eval_jaxpr/all_gather | solution.py:84
  411.8 0.7 conditional.4
  411.8 0.7 broadcast_in_dim.2
  412.5 0.2 copy-done.1
  412.8 1.1 convert_add_fusion
  413.9 0.0 copy-start.2
  413.9 0.3 multiply_convert_fusion
  414.3 4.0 collective-permute-start.2
  418.3 1.3 collective-permute-start.3
  420.3 1.5 collective-permute-done.3
  421.8 4.1 collective-permute-start.4
  425.8 1.9 collective-permute-start.5
  427.8 0.1 multiply_add_fusion
  427.9 5.4 %collective-permute-done.5 = bf16[6,1,512]{2,1,0:T(2,128)(2,1)S(1)} collective-permute-done((bf16[6,1,512]{2,1,0:T(2,128)(2,1)S(1)}, bf16[6,1,512]{2,1,0:T(2,128)(2,1)S(1)}, u32[]{:S(2)}, u32[]{:S(2)}) %collective-permute-start.5) | collective-permute-done | bytes 6176 | tf_op jit(solution)/shard_map/ppermute | solution.py:25
  433.2 0.6 maximum_convert_fusion
  433.8 2.1 fusion.2
  (30 shorter events, 0.3 us)
Async XLA Ops:
  7.3 70.0 %all-gather.5.cloned.1.call-start = ((), (), s32[]{:S(2)}) async-start(), calls=%async_computation.1 | async-start | bytes 2506752 | tf_op jit(solution)/shard_map/while/body/eval_jaxpr/all_gather | solution.py:87
  7.3 4.4 collective-permute-start
  8.7 4.2 collective-permute-start.1
  14.7 126.0 %all-gather.3.cloned.1.call-start = ((), (), s32[]{:S(2)}) async-start(), calls=%async_computation | async-start | bytes 2506752 | tf_op jit(solution)/shard_map/while/body/eval_jaxpr/all_gather | solution.py:84
  77.3 63.4 %copy-start.3 = (bf16[288,4608]{1,0:T(8,128)(2,1)S(1)}, bf16[288,4608]{1,0:T(8,128)(2,1)}, u32[]{:S(2)}) copy-start(bf16[288,4608]{1,0:T(8,128)(2,1)} %get-tuple-element.335) | copy-start | bytes 7962628 | tf_op jit(solution)/shard_map/while
  77.3 0.7 copy-start
  140.7 4.2 copy-start.1
  144.9 68.1 %all-gather.5.cloned.1.call-start = ((), (), s32[]{:S(2)}) async-start(), calls=%async_computation.1 | async-start | bytes 2506752 | tf_op jit(solution)/shard_map/while/body/eval_jaxpr/all_gather | solution.py:87
  145.0 4.4 collective-permute-start
  146.3 4.2 collective-permute-start.1
  152.3 124.0 %all-gather.3.cloned.1.call-start = ((), (), s32[]{:S(2)}) async-start(), calls=%async_computation | async-start | bytes 2506752 | tf_op jit(solution)/shard_map/while/body/eval_jaxpr/all_gather | solution.py:84
  213.0 63.3 %copy-start.3 = (bf16[288,4608]{1,0:T(8,128)(2,1)S(1)}, bf16[288,4608]{1,0:T(8,128)(2,1)}, u32[]{:S(2)}) copy-start(bf16[288,4608]{1,0:T(8,128)(2,1)} %get-tuple-element.335) | copy-start | bytes 7962628 | tf_op jit(solution)/shard_map/while
  216.5 0.7 copy-start
  276.3 4.2 copy-start.1
  280.5 68.1 %all-gather.5.cloned.1.call-start = ((), (), s32[]{:S(2)}) async-start(), calls=%async_computation.1 | async-start | bytes 2506752 | tf_op jit(solution)/shard_map/while/body/eval_jaxpr/all_gather | solution.py:87
  280.5 4.4 collective-permute-start
  281.8 4.2 collective-permute-start.1
  287.8 124.0 %all-gather.3.cloned.1.call-start = ((), (), s32[]{:S(2)}) async-start(), calls=%async_computation | async-start | bytes 2506752 | tf_op jit(solution)/shard_map/while/body/eval_jaxpr/all_gather | solution.py:84
  348.6 63.3 %copy-start.3 = (bf16[288,4608]{1,0:T(8,128)(2,1)S(1)}, bf16[288,4608]{1,0:T(8,128)(2,1)}, u32[]{:S(2)}) copy-start(bf16[288,4608]{1,0:T(8,128)(2,1)} %get-tuple-element.335) | copy-start | bytes 7962628 | tf_op jit(solution)/shard_map/while
  352.0 0.7 copy-start
  411.8 1.0 copy-start.1
  413.9 13.9 %copy-start.2 = (s32[4,288]{1,0:T(4,128)S(1)}, s32[4,288]{1,0:T(4,128)}, u32[]{:S(2)}) copy-start(s32[4,288]{1,0:T(4,128)} %param.14) | copy-start | bytes 13828
  414.3 6.0 %collective-permute-start.2 = (bf16[1,288,512]{2,1,0:T(8,128)(2,1)S(1)}, bf16[1,288,512]{2,1,0:T(8,128)(2,1)S(1)}, u32[]{:S(2)}, u32[]{:S(2)}) collective-permute-start(bf16[1,288,512]{2,1,0:T(8,128)(2,1)S(1)} %get-tuple-element.229), channel_id=1, source_target_pairs={{0,16},{1,17},{2,18},{3,19},{4,20},{5,21},{6,22},{7,23},{8,24},{9,... | collective-permute-start | bytes 884744 | tf_op jit(solution)/shard_map/ppermute | solution.py:23
  418.3 3.5 collective-permute-start.3
  421.8 6.1 %collective-permute-start.4 = (bf16[6,1,512]{2,1,0:T(2,128)(2,1)S(1)}, bf16[6,1,512]{2,1,0:T(2,128)(2,1)S(1)}, u32[]{:S(2)}, u32[]{:S(2)}) collective-permute-start(bf16[6,1,512]{2,1,0:T(2,128)(2,1)S(1)} %get-tuple-element.227), channel_id=1, source_target_pairs={{0,1},{1,2},{2,3},{3,4},{4,5},{5,6},{6,7},{7,8},{8,9},{9,10},{10,1... | collective-permute-start | bytes 18440 | tf_op jit(solution)/shard_map/ppermute | solution.py:23
  425.8 7.4 %collective-permute-start.5 = (bf16[6,1,512]{2,1,0:T(2,128)(2,1)S(1)}, bf16[6,1,512]{2,1,0:T(2,128)(2,1)S(1)}, u32[]{:S(2)}, u32[]{:S(2)}) collective-permute-start(bf16[6,1,512]{2,1,0:T(2,128)(2,1)S(1)} %get-tuple-element.228), channel_id=1, source_target_pairs={{1,0},{2,1},{3,2},{4,3},{5,4},{6,5},{7,6},{8,7},{9,8},{10,9},{11,1... | collective-permute-start | bytes 18440 | tf_op jit(solution)/shard_map/ppermute | solution.py:25
Sparse Core Ops, SparseCore 0:
  14.8 62.4 all-gather.4
  80.1 60.5 all-gather.2
  152.4 60.5 all-gather.4
  215.7 60.5 all-gather.2
  288.0 60.5 all-gather.4
  351.2 60.5 all-gather.2
where the time goes:
time: 443 us
  waiting for transfers between devices  373 us (84%)
  starting transfers between devices  24.5 us (6%)
  between operations  14.1 us (3%)
  other arithmetic  13.4 us (3%)
  matrix products  13.3 us (3%)
    all_gather x3, waiting for transfers between devices, both_step(): lax.all_gather(entry_up, 'row', axis=0, tiled=True)  182 us
    all_gather x3, waiting for transfers between devices, both_step(): lax.all_gather(entry_down, 'row', axis=0, tiled=True)  179 us
    dot_general x4, matrix products, folder(): jnp.dot(matrix, piece, preferred_element_type=jnp.float32)  13.3 us
    ppermute x6, starting transfers between devices, shifted(): lax.ppermute(value, axis, [(source, source + steps) for source in range(l...  13 us
  transfers between devices with their start and end apart: 16, of which 11 were waited for; matrix products, arithmetic and copies ran while one was open for 2% of the time, Pallas kernels for 0%

commit v1 on v0

v1 whole, which is shorter than its diff:
```python
import jax
import jax.numpy as jnp
from jax import lax
from jax.sharding import PartitionSpec as P


def shifted(value, axis, steps):
    count = lax.axis_size(axis)
    leading, last = (max(0, -steps), min(count, count - steps))
    return lax.ppermute(value, axis, [(source, source + steps) for source in range(leading, last)])


def ramp(index, count, thick):
    dist = jnp.minimum(index, count - 1 - index).astype(jnp.float32)
    return jnp.maximum(thick - dist, 0.0) / thick


def gather(block):
    return lax.all_gather(block, "row", axis=0, tiled=True)


def residual_of(source, first, second, material, pml_cells, here, layers):
    rows, total = source.shape
    planes = material.shape[0]
    wave = source.astype(jnp.float32) + first.astype(jnp.float32) + second.astype(jnp.float32)
    factor = (planes - jnp.arange(planes, dtype=jnp.float32)) / planes
    sent = wave.astype(jnp.bfloat16)
    other = sent[None]
    before_plane = shifted(other, "layer", 1).astype(jnp.float32) * factor[planes - 1]
    after_plane = shifted(other, "layer", -1).astype(jnp.float32) * factor[0]
    before_row = shifted(sent[rows - 1 :], "row", 1).astype(jnp.float32)
    after_row = shifted(sent[:1], "row", -1).astype(jnp.float32)
    thick = pml_cells[0].astype(jnp.float32)
    plane_index = here * planes + jnp.arange(planes, dtype=jnp.int32)
    point_index = lax.axis_index("row") * rows + jnp.arange(rows, dtype=jnp.int32)
    ramp_z = ramp(plane_index, layers * planes, thick)
    ramp_m = ramp(point_index, rows * lax.axis_size("row"), thick)
    sigma = 3.0 * (ramp_z[:, None] * ramp_z[:, None] + ramp_m[None, :] * ramp_m[None, :])
    kappa = 1.0 + 1.5 * material.astype(jnp.float32)
    slab = wave[None] * factor[:, None, None]
    tall = jnp.concatenate([before_plane, slab, after_plane], axis=0)
    wide = jnp.concatenate([before_row, wave, after_row], axis=0)
    beside_rows = (wide[2:] + wide[:-2])[None] * factor[:, None, None]
    beside = tall[2:] + tall[:-2] + beside_rows
    result = kappa[:, :, None] * ((4.0 + sigma)[:, :, None] * slab - beside)
    return result.astype(jnp.bfloat16)


def local(sources, green_down, green_up, material, pml_cells):
    source = sources[0]
    layers = lax.axis_size("layer")
    here = lax.axis_index("layer")

    def multiply(pick_down, block):
        def with_matrix(matrix):
            return lambda: jnp.dot(matrix[0], block, preferred_element_type=jnp.float32)

        return lax.cond(pick_down, with_matrix(green_down), with_matrix(green_up)).astype(jnp.bfloat16)

    first = multiply(here == 0, gather(source))
    moved = lax.ppermute(first, "layer", [(0, 1), (1, 0)])
    entry = (source.astype(jnp.float32) + moved.astype(jnp.float32)).astype(jnp.bfloat16)
    second = multiply(here != 0, gather(entry))
    return residual_of(source, first, second, material, pml_cells, here, layers)


def solution(mesh):
    return jax.shard_map(
        local,
        mesh=mesh,
        in_specs=(
            P("layer", "row", None),
            P("layer", "row", None),
            P("layer", "row", None),
            P("layer", "row"),
            P(),
        ),
        out_specs=P("layer", "row", None),
        check_vma=False,
    )
```

time: 443 us -> 205 us (0.46)
  waiting for transfers between devices: 373 us -> 163 us
  starting transfers between devices: 24.5 us -> 10.4 us
  other arithmetic: 13.4 us -> 4.42 us
    all_gather x6 -> x2, waiting for transfers between devices: 361 us -> 160 us  [gather(): return lax.all_gather(block, 'row', axis=0, tiled=True)]
    ppermute x4 -> x1, starting transfers between devices: 11.3 us -> 0.07 us  [local(): moved = lax.ppermute(first, 'layer', [(0, 1), (1, 0)])]
    convert_element_type x6 -> x5, other arithmetic: 8.3 us -> 2.47 us  [the longest x1 1.55 us: residual_of(): return result.astype(jnp.bfloat16)]
    ppermute x4 -> x1, waiting for transfers between devices: 6.85 us -> 1.57 us  [local(): moved = lax.ppermute(first, 'layer', [(0, 1), (1, 0)])]
    dot_general x4 -> x2, matrix products: 13.3 us -> 9.37 us  [with_matrix(): return lambda: jnp.dot(matrix[0], block, preferred_element_type=jnp.float32)]
    ppermute x6 -> x4, starting transfers between devices: 13 us -> 10.2 us  [shifted(): lax.ppermute(value, axis, [(source, source + steps) for source in range(l...]
  transfers between devices with their start and end apart: 16 -> 7, of which waited for: 11 -> 4; matrix products, arithmetic and copies ran while one was open for 2% -> 1% of each run, Pallas kernels for 0% -> 0%
where the time goes in v1:
time: 205 us; the launch traced here: 202 us
  waiting for transfers between devices  163 us (80%)
  between operations  14.2 us (7%)
  starting transfers between devices  10.4 us (5%)
  matrix products  9.37 us (5%)
  other arithmetic  4.42 us (2%)
    all_gather x2, waiting for transfers between devices, gather(): return lax.all_gather(block, 'row', axis=0, tiled=True)  160 us
    ppermute x4, starting transfers between devices, shifted(): lax.ppermute(value, axis, [(source, source + steps) for source in range(l...  10.2 us
    dot_general x2, matrix products, with_matrix(): return lambda: jnp.dot(matrix[0], block, preferred_element_type=jnp.float32)  9.37 us
  transfers between devices with their start and end apart: 7, of which 4 were waited for; matrix products, arithmetic and copies ran while one was open for 1% of the time, Pallas kernels for 0%

profile of v1, /device:TPU:6, one launch (start us, length us, event | category | flops | bytes accessed | tf_op | source)
XLA Modules:
  0.0 202.1 jit_solution(5933260169027797357)
XLA Ops:
  6.5 0.0 all-gather.6.cloned.1.call-start
  6.5 0.7 all-gather.6.cloned.1.call-update
  7.3 0.0 all-gather.4.cloned.1.call-start
  7.3 82.8 %all-gather.6.cloned.1.call-done = bf16[1,4608,512]{2,1,0:T(8,128)(2,1)} async-done(((bf16[1,288,512]{2,1,0:T(8,128)(2,1)}), bf16[1,4608,512]{2,1,0:T(8,128)(2,1)}) %all-gather.6.cloned.1.call-update) | async-done | bytes 4718608 | tf_op jit(solution)/shard_map/all_gather | solution.py:19
  90.1 0.0 copy-start
  90.1 0.0 copy-start.1
  90.1 4.7 %conditional.2 = (bf16[288,512]{1,0:T(8,128)(2,1)S(1)}) conditional(s32[]{:T(128)} %convert_element_type.75, (bf16[1,288,4608]{2,1,0:T(8,128)(2,1)}, bf16[4608,512]{1,0:T(8,128)(2,1)}) %tuple.33, (bf16[1,288,4608]{2,1,0:T(8,128)(2,1)}, bf16[4608,512]{1,0:T(8,128)(2,1)}) %tuple.34), branch_computations={%region_0.0_spmd, %region_1.0_spmd} | conditional | flops 1358954496 | bytes 7667720 | solution.py:58
  90.1 4.7 %fusion.2 = bf16[288,512]{1,0:T(8,128)(2,1)S(1)} fusion(bf16[4608,512]{1,0:T(8,128)(2,1)} %get-tuple-element.30, bf16[1,288,4608]{2,1,0:T(8,128)(2,1)} %get-tuple-element.29), kind=kOutput, calls=%fused_computation.2 | convolution fusion | flops 1358954496 | bytes 7667712 | tf_op jit(solution)/shard_map/cond/branch_1_fun/dot_general | solution.py:56
  94.8 0.1 collective-permute-start
  94.9 1.6 collective-permute-done
  96.5 0.0 copy-done
  96.5 0.8 fusion.14
  97.3 0.0 all-gather.4.cloned.1.call-update
  98.0 0.6 fusion.25
  98.6 0.0 copy-done.1
  98.7 0.1 multiply_add_fusion
  98.7 77.1 %all-gather.4.cloned.1.call-done = bf16[4608,512]{1,0:T(8,128)(2,1)} async-done(((bf16[288,512]{1,0:T(8,128)(2,1)}), bf16[4608,512]{1,0:T(8,128)(2,1)}) %all-gather.4.cloned.1.call-update) | async-done | bytes 4718608 | tf_op jit(solution)/shard_map/all_gather | solution.py:19
  175.8 4.7 %conditional.3 = (bf16[288,512]{1,0:T(8,128)(2,1)S(1)}) conditional(s32[]{:T(128)} %convert_element_type.78, (bf16[1,288,4608]{2,1,0:T(8,128)(2,1)}, bf16[4608,512]{1,0:T(8,128)(2,1)}) %tuple.19, (bf16[1,288,4608]{2,1,0:T(8,128)(2,1)}, bf16[4608,512]{1,0:T(8,128)(2,1)}) %tuple.20), branch_computations={%region_2.0_spmd, %region_3.0_spmd} | conditional | flops 1358954496 | bytes 7667720 | solution.py:58
  175.8 4.7 %fusion.4 = bf16[288,512]{1,0:T(8,128)(2,1)S(1)} fusion(bf16[4608,512]{1,0:T(8,128)(2,1)} %get-tuple-element.32, bf16[1,288,4608]{2,1,0:T(8,128)(2,1)} %get-tuple-element.31), kind=kOutput, calls=%fused_computation.4 | convolution fusion | flops 1358954496 | bytes 7667712 | tf_op jit(solution)/shard_map/cond/branch_0_fun/dot_general | solution.py:56
  180.5 0.1 fusion.22
  180.6 1.3 collective-permute-start.2
  181.9 1.3 collective-permute-start.1
  183.2 3.4 %collective-permute-start.3 = (bf16[1,512]{1,0:T(2,128)(2,1)S(1)}, bf16[1,512]{1,0:T(2,128)(2,1)S(1)}, u32[]{:S(2)}, u32[]{:S(2)}) collective-permute-start(bf16[1,512]{1,0:T(2,128)(2,1)S(1)} %get-tuple-element.37), channel_id=1, source_target_pairs={{1,0},{2,1},{3,2},{4,3},{5,4},{6,5},{7,6},{8,7},{9,8},{10,9},{11,1... | collective-permute-start | bytes 3080 | tf_op jit(solution)/shard_map/ppermute | solution.py:10
  186.6 4.3 %collective-permute-start.4 = (bf16[1,512]{1,0:T(2,128)(2,1)S(1)}, bf16[1,512]{1,0:T(2,128)(2,1)S(1)}, u32[]{:S(2)}, u32[]{:S(2)}) collective-permute-start(bf16[1,512]{1,0:T(2,128)(2,1)S(1)} %get-tuple-element.38), channel_id=1, source_target_pairs={{0,1},{1,2},{2,3},{3,4},{4,5},{5,6},{6,7},{7,8},{8,9},{9,10},{10,1... | collective-permute-start | bytes 3080 | tf_op jit(solution)/shard_map/ppermute | solution.py:10
  190.9 0.4 broadcast_multiply_fusion
  191.3 0.0 collective-permute-done.3
  191.3 0.9 collective-permute-done.4
  192.2 0.1 fusion.15
  192.3 0.0 collective-permute-done.2
  192.3 0.7 convert_multiply_fusion
  193.0 0.0 collective-permute-done.1
  193.0 0.7 convert_multiply_fusion.1
  193.7 1.6 fusion.12
  (6 shorter events, 0.1 us)
Async XLA Ops:
  6.5 83.6 %all-gather.6.cloned.1.call-start = ((), (), s32[]{:S(2)}) async-start(), calls=%async_computation.1 | async-start | bytes 5013504 | tf_op jit(solution)/shard_map/all_gather | solution.py:19
  7.3 168.5 %all-gather.4.cloned.1.call-start = ((), (), s32[]{:S(2)}) async-start(), calls=%async_computation | async-start | bytes 5013504 | tf_op jit(solution)/shard_map/all_gather | solution.py:19
  90.1 6.4 %copy-start = (bf16[1,288,512]{2,1,0:T(8,128)(2,1)S(1)}, bf16[1,288,512]{2,1,0:T(8,128)(2,1)}, u32[]{:S(2)}) copy-start(bf16[1,288,512]{2,1,0:T(8,128)(2,1)} %param.9) | copy-start | bytes 884740
  90.1 8.5 %copy-start.1 = (s32[4,288]{1,0:T(4,128)S(1)}, s32[4,288]{1,0:T(4,128)}, u32[]{:S(2)}) copy-start(s32[4,288]{1,0:T(4,128)} %param.12) | copy-start | bytes 13828
  94.8 1.6 collective-permute-start
  180.6 11.7 %collective-permute-start.2 = (bf16[1,288,512]{2,1,0:T(8,128)(2,1)S(1)}, bf16[1,288,512]{2,1,0:T(8,128)(2,1)S(1)}, u32[]{:S(2)}, u32[]{:S(2)}) collective-permute-start(bf16[1,288,512]{2,1,0:T(8,128)(2,1)S(1)} %bitcast.26), channel_id=1, source_target_pairs={{0,16},{1,17},{2,18},{3,19},{4,20},{5,21},{6,22},{7,23},{8,24},{9,... | collective-permute-start | bytes 884744 | tf_op jit(solution)/shard_map/ppermute | solution.py:10
  181.9 11.1 %collective-permute-start.1 = (bf16[1,288,512]{2,1,0:T(8,128)(2,1)S(1)}, bf16[1,288,512]{2,1,0:T(8,128)(2,1)S(1)}, u32[]{:S(2)}, u32[]{:S(2)}) collective-permute-start(bf16[1,288,512]{2,1,0:T(8,128)(2,1)S(1)} %bitcast.27), channel_id=1, source_target_pairs={{16,0},{17,1},{18,2},{19,3},{20,4},{21,5},{22,6},{23,7},{24,8},{25... | collective-permute-start | bytes 884744 | tf_op jit(solution)/shard_map/ppermute | solution.py:10
  183.2 8.0 %collective-permute-start.3 = (bf16[1,512]{1,0:T(2,128)(2,1)S(1)}, bf16[1,512]{1,0:T(2,128)(2,1)S(1)}, u32[]{:S(2)}, u32[]{:S(2)}) collective-permute-start(bf16[1,512]{1,0:T(2,128)(2,1)S(1)} %get-tuple-element.37), channel_id=1, source_target_pairs={{1,0},{2,1},{3,2},{4,3},{5,4},{6,5},{7,6},{8,7},{9,8},{10,9},{11,1... | collective-permute-start | bytes 3080 | tf_op jit(solution)/shard_map/ppermute | solution.py:10
  186.6 5.6 %collective-permute-start.4 = (bf16[1,512]{1,0:T(2,128)(2,1)S(1)}, bf16[1,512]{1,0:T(2,128)(2,1)S(1)}, u32[]{:S(2)}, u32[]{:S(2)}) collective-permute-start(bf16[1,512]{1,0:T(2,128)(2,1)S(1)} %get-tuple-element.38), channel_id=1, source_target_pairs={{0,1},{1,2},{2,3},{3,4},{4,5},{5,6},{6,7},{7,8},{8,9},{9,10},{10,1... | collective-permute-start | bytes 3080 | tf_op jit(solution)/shard_map/ppermute | solution.py:10
Sparse Core Ops, SparseCore 0:
  10.1 79.9 all-gather.5
  97.4 78.3 all-gather.3
